TPU v7x, 32 devices: a whole 2x2x4 slice. The times are simulated.
32 devices in a mesh: expert: 8 (over z, core), row: 4 (over y, x).
Axes of the slice: x: 2, y: 2, z: 4, core: 2. Of those that a mesh axis runs over, the one named last changes fastest.
Arguments:
- grads: bfloat16 [8, 7168, 2048], P('expert', 'row')
- basis: bfloat16 [8, 7168, 256], P('expert', 'row'), may hold values from -0.0625 to 0.0625
- loads: int32 [8], P('expert'), may hold values from 1 to 1, as said below
- flags: int32 [8], P('expert'), may hold values 0 or 1
Outputs:
- new_basis: float32 [8, 7168, 256], P('expert', 'row')
- rotated: float32 [8, 256, 2048], P('expert', None, 'row')
Inputs may be any that keep to these rules, and one draw needn't show every extreme that they name: Slots 0 to loads[d] - 1 of expert-axis index d are live and hold experts; the others are empty. Some index has all 1 slots live.
All inputs are finite; a program needn't handle non-finite values. No bound on the sum of `flags` on one device may be relied on, other than what follows from the above.
Results may differ from a plain program's by a relative error of at most 0.006.
Values sent between devices are 32-bit elements; how exact they have to be, the bound alone decides.
A program may use at most 64 MiB of HBM per device.

v0:
```python
import jax
import jax.numpy as jnp
from jax import lax
from jax.sharding import PartitionSpec as P

D = 7168
S = 2048


def on_device(grads, basis, loads, flags):
    slot_count = grads.shape[0]
    live_count = loads[0]
    live_mask = jnp.arange(slot_count, dtype=jnp.int32) < live_count
    refresh = jnp.logical_and(live_mask, flags == 1)
    live_cube = live_mask[:, None, None]
    refresh_cube = refresh[:, None, None]
    squares = jnp.sum(jnp.where(live_cube, jnp.square(grads.astype(jnp.float32)), 0.0))
    leader = (lax.axis_index("row") == 0).astype(jnp.float32)
    total_sq, total_live = lax.psum(
        (squares, leader * live_count.astype(jnp.float32)), ("expert", "row")
    )
    norm_scale = lax.rsqrt(total_sq / (total_live * D * S) + 1e-06)
    local_inner = jnp.einsum("cds,cdk->csk", grads, basis, preferred_element_type=jnp.float32)
    inner_sum = jnp.stack([lax.psum(local_inner[0], "row")])
    inner_gram = jnp.einsum("csk,csj->ckj", inner_sum, inner_sum, precision=lax.Precision.HIGHEST)
    inner_half = inner_sum.astype(jnp.bfloat16)
    power_rows = jnp.einsum(
        "cds,csk->cdk", grads, inner_half, preferred_element_type=jnp.float32
    ).astype(jnp.bfloat16)
    projector = jnp.where(refresh_cube, power_rows, basis)
    local_cross = jnp.einsum("cdk,cds->cks", projector, grads, preferred_element_type=jnp.float32)
    identity = jnp.eye(basis.shape[2], dtype=jnp.float32)
    lower_first = jnp.linalg.cholesky(jnp.where(refresh_cube, inner_gram, identity))
    first_rows = lax.linalg.triangular_solve(
        lower_first, power_rows.astype(jnp.float32), left_side=False, lower=True, transpose_a=True
    )
    local_second = jnp.einsum(
        "cdk,cdj->ckj", first_rows, first_rows, precision=lax.Precision.HIGHEST
    )
    gram_again = lax.psum(local_second, "row")
    cross_cols = lax.psum_scatter(local_cross, "row", scatter_dimension=2, tiled=True)
    lower_second = jnp.linalg.cholesky(jnp.where(refresh_cube, gram_again, identity))
    fresh_basis = lax.linalg.triangular_solve(
        lower_second, first_rows, left_side=False, lower=True, transpose_a=True
    )
    half_solved = lax.linalg.triangular_solve(lower_first, cross_cols, left_side=True, lower=True)
    fresh_rot = lax.linalg.triangular_solve(lower_second, half_solved, left_side=True, lower=True)
    new_basis = jnp.where(
        refresh_cube, fresh_basis, jnp.where(live_cube, basis.astype(jnp.float32), 0.0)
    )
    rotated = jnp.where(refresh_cube, fresh_rot, jnp.where(live_cube, cross_cols, 0.0)) * norm_scale
    return (new_basis, rotated)


def solution(mesh):
    placed = (P("expert", "row", None), P("expert", "row", None), P("expert"), P("expert"))
    return jax.shard_map(
        on_device,
        mesh=mesh,
        in_specs=placed,
        out_specs=(P("expert", "row", None), P("expert", None, "row")),
        check_vma=False,
    )
```

profile of v0, /device:TPU:0, one launch (start us, length us, event | category | flops | bytes accessed | tf_op | source)
XLA Modules:
  0.0 307.3 jit_solution(6141670956639925859)
XLA Ops:
  7.2 6.8 %fusion.4 = f32[2048,256]{1,0:T(8,128)} fusion(bf16[1,1792,2048]{2,1,0:T(8,128)(2,1)} %param.9, bf16[1,1792,256]{2,1,0:T(8,128)(2,1)} %param.10), kind=kOutput, calls=%fused_computation.9 | convolution fusion | flops 1879048192 | bytes 10354688 | tf_op jit(solution)/shard_map/cds,cdk->csk/dot_general | solution.py:23
  14.1 1.1 copy-done.2
  15.2 1.1 copy.12
  17.7 68.7 %all-reduce.5.cloned.1.call-done = f32[2048,256]{1,0:T(8,128)} async-done(((f32[2048,256]{1,0:T(8,128)}), f32[2048,256]{1,0:T(8,128)}) %all-reduce.5.cloned.1.call-update) | async-done | bytes 2097168 | tf_op jit(solution)/shard_map/psum | solution.py:24
  86.4 5.7 %convolution_select_fusion = f32[256,256]{0,1:T(8,128)S(1)} fusion(f32[2048,256]{1,0:T(8,128)} %all-reduce.5.cloned.1.call-done, pred[]{:T(512)} %bitcast), kind=kOutput, calls=%fused_computation.32 | convolution fusion | flops 1610809344 | bytes 2359297 | tf_op jit(solution)/shard_map/csk,csj->ckj/dot_general | solution.py:25
  92.3 0.7 copy-done.3
  93.0 11.7 %custom-call.21 = f32[1,128,128]{2,1,0:T(8,128)S(1)} custom-call(f32[1,128,128]{2,1,0:T(8,128)S(1)} %cholesky.191), custom_call_target="Cholesky" | custom-call | tf_op jit(solution)/shard_map/jit(cholesky)/cholesky | solution.py:33
  104.7 9.8 %custom-call.22 = f32[1,1,128,128]{2,3,1,0:T(8,128)S(1)} custom-call(f32[1,1,128,128]{3,2,1,0:T(8,128)S(1)} %get-tuple-element.68), custom_call_target="InvertDiagBlocksLowerTriangular" | custom-call | tf_op jit(solution)/shard_map/jit(cholesky)/cholesky | solution.py:33
  114.6 1.0 bitcast_dynamic-update-slice_fusion.3
  115.6 1.1 fusion.27
  116.7 11.9 %custom-call.23 = f32[1,128,128]{2,1,0:T(8,128)S(1)} custom-call(f32[1,128,128]{2,1,0:T(8,128)S(1)} %fusion.27), custom_call_target="Cholesky" | custom-call | tf_op jit(solution)/shard_map/jit(cholesky)/cholesky | solution.py:33
  128.6 0.7 compare_reduce_fusion.2
  130.7 3.9 %while.8 = (s32[]{:T(128)}, f32[1,256,256]{2,1,0:T(8,128)S(1)}, s32[2,2]{1,0:T(2,128)S(1)}, f32[2,1,128,128]{3,2,1,0:T(8,128)S(1)}, s32[]{:T(128)}) while((s32[]{:T(128)}, f32[1,256,256]{2,1,0:T(8,128)S(1)}, s32[2,2]{1,0:T(2,128)S(1)}, f32[2,1,128,128]{3,2,1,0:T(8,128)S(1)}, s32[]{:T(128)}) %tuple.57), condition=%wide.while_cond, body=%wide.while_body.sunk | while | flops 2 | bytes 131181 | solution.py:34
  130.7 0.6 fusion.71
  131.3 1.4 bitcast_dynamic-update-slice_fusion.6
  132.7 0.6 fusion.71
  133.3 1.4 bitcast_dynamic-update-slice_fusion.6
  134.6 19.7 %custom-call.24 = f32[1,2,128,128]{2,3,1,0:T(8,128)S(1)} custom-call(f32[1,2,128,128]{3,2,1,0:T(8,128)S(1)} %bitcast.221), custom_call_target="InvertDiagBlocksLowerTriangular" | custom-call | tf_op jit(solution)/shard_map/triangular_solve/custom-call.0 | solution.py:34
  154.3 6.2 %fusion.53 = (f32[1,1792,256]{1,2,0:T(8,128)S(1)}, bf16[1,1792,256]{1,2,0:T(8,128)(2,1)}) fusion(bf16[1,1792,2048]{2,1,0:T(8,128)(2,1)} %param.9, f32[2048,256]{1,0:T(8,128)S(1)} %copy-done), kind=kOutput, calls=%fused_computation.99 | convolution fusion | flops 1880489984 | bytes 12189696 | tf_op jit(solution)/shard_map/cds,csk->cdk/dot_general | solution.py:27
  160.5 1.0 fusion.30
  161.5 1.0 fusion.16
  162.5 1.0 convolution_bitcast_fusion.2
  163.4 2.4 fusion.22
  165.9 6.8 %fusion.6 = f32[1,256,2048]{2,1,0:T(8,128)} fusion(bf16[1,1792,2048]{2,1,0:T(8,128)(2,1)} %param.9, bf16[1,1792,256]{1,2,0:T(8,128)(2,1)} %get-tuple-element.70, bf16[1,1792,256]{1,2,0:T(8,128)(2,1)S(1)} %copy.12, pred[]{:T(512)} %bitcast), kind=kOutput, calls=%fused_computation.11 | convolution fusion | flops 1879506944 | bytes 11272193 | tf_op jit(solution)/shard_map/cdk,cds->cks/dot_general | solution.py:31
  172.7 7.5 %select_reduce_fusion = f32[]{:T(128)} fusion(bf16[1,1792,2048]{2,1,0:T(8,128)(2,1)} %param.9, pred[]{:T(512)} %bitcast.40), kind=kLoop, calls=%fused_computation.4 | loop fusion | flops 14680063 | bytes 7340037 | tf_op jit(solution)/shard_map/reduce_sum | solution.py:17
  180.2 39.4 %all-reduce.1 = (f32[]{:T(128)}, f32[]{:T(128)}) all-reduce(f32[]{:T(128)} %select_reduce_fusion, f32[]{:T(128)S(6)} %mul.13), channel_id=1, replica_groups=mesh['expert'=8,'row'=4] {'expert','row'}, use_global_device_ids=true, to_apply=%region_8.12 | all-reduce | flops 2 | bytes 16 | tf_op jit(solution)/shard_map/psum | solution.py:19
  221.0 1.0 convert_select_fusion
  222.1 1.0 fusion.40
  223.1 12.3 %custom-call.25 = f32[1,128,128]{2,1,0:T(8,128)} custom-call(f32[1,128,128]{2,1,0:T(8,128)S(1)} %cholesky.194), custom_call_target="Cholesky" | custom-call | tf_op jit(solution)/shard_map/jit(cholesky)/cholesky | solution.py:42
  235.5 0.9 cholesky.185
  236.3 1.5 select_reduce_fusion.2
  237.8 11.3 %custom-call.26 = f32[1,1,128,128]{2,3,1,0:T(8,128)} custom-call(f32[1,1,128,128]{3,2,1,0:T(8,128)} %get-tuple-element.64), custom_call_target="InvertDiagBlocksLowerTriangular" | custom-call | tf_op jit(solution)/shard_map/jit(cholesky)/cholesky | solution.py:42
  249.1 1.0 bitcast_dynamic-update-slice_fusion.2
  250.2 0.9 fusion.28
  251.1 12.5 %custom-call.27 = f32[1,128,128]{2,1,0:T(8,128)S(1)} custom-call(f32[1,128,128]{2,1,0:T(8,128)} %fusion.28), custom_call_target="Cholesky" | custom-call | tf_op jit(solution)/shard_map/jit(cholesky)/cholesky | solution.py:42
  263.7 0.6 compare_reduce_fusion
  264.3 0.6 compare_reduce_fusion.1
  266.3 4.0 %while.9 = (s32[]{:T(128)}, f32[1,256,256]{2,1,0:T(8,128)S(1)}, s32[2,2]{1,0:T(2,128)S(1)}, f32[2,1,128,128]{3,2,1,0:T(8,128)S(1)}, s32[]{:T(128)}) while((s32[]{:T(128)}, f32[1,256,256]{2,1,0:T(8,128)S(1)}, s32[2,2]{1,0:T(2,128)S(1)}, f32[2,1,128,128]{3,2,1,0:T(8,128)S(1)}, s32[]{:T(128)}) %tuple.69), condition=%wide.while_cond.clone, body=%wide.while_body.clone.sunk | while | flops 2 | bytes 131181 | solution.py:43
  266.9 1.4 bitcast_dynamic-update-slice_fusion.7
  268.9 1.4 bitcast_dynamic-update-slice_fusion.7
  270.3 19.9 %custom-call.28 = f32[1,2,128,128]{2,3,1,0:T(8,128)S(1)} custom-call(f32[1,2,128,128]{3,2,1,0:T(8,128)S(1)} %bitcast.220), custom_call_target="InvertDiagBlocksLowerTriangular" | custom-call | tf_op jit(solution)/shard_map/triangular_solve/custom-call.0 | solution.py:43
  290.2 0.9 fusion.31
  291.2 1.0 fusion.18
  292.1 1.0 convolution_bitcast_fusion
  293.3 1.7 copy.14
  295.0 1.4 fusion.38
  297.3 1.3 fusion.24
  299.5 0.9 fusion.37
  (44 shorter events, 3.8 us)
Async XLA Ops:
  7.2 79.2 %all-reduce.5.cloned.1.call-start = ((), (), s32[]{:S(2)}) async-start(), calls=%async_computation.1 | async-start | bytes 4194304 | tf_op jit(solution)/shard_map/psum | solution.py:24
  14.0 1.2 copy-start.2
  14.1 206.9 %all-reduce.7.cloned.1.call-start = ((), (), s32[]{:S(2)}) async-start(), calls=%async_computation.2 | async-start | bytes 524288 | tf_op jit(solution)/shard_map/psum | solution.py:40
  92.1 62.3 %copy-start = (f32[2048,256]{1,0:T(8,128)S(1)}, f32[2048,256]{1,0:T(8,128)}, u32[]{:S(2)}) copy-start(f32[2048,256]{1,0:T(8,128)} %all-reduce.5.cloned.1.call-done) | copy-start | bytes 6291460
  92.3 0.7 copy-start.3
  154.3 8.1 %copy-start.4 = (f32[1,2,128,128]{2,3,1,0:T(8,128)}, f32[1,2,128,128]{2,3,1,0:T(8,128)S(1)}, u32[]{:S(2)}) copy-start(f32[1,2,128,128]{2,3,1,0:T(8,128)S(1)} %custom-call.24) | copy-start | bytes 393220
  165.8 129.2 %reduce-scatter.2.cloned.1.call-start = ((), (), s32[]{:S(2)}) async-start(), calls=%async_computation.3 | async-start | bytes 2621440 | tf_op jit(solution)/shard_map/reduce_scatter | solution.py:41
  293.3 1.7 copy-start.5
  295.0 4.4 %copy-start.1 = (f32[1,256,512]{2,1,0:T(8,128)S(1)}, f32[1,256,512]{2,1,0:T(8,128)}, u32[]{:S(2)}) copy-start(f32[1,256,512]{2,1,0:T(8,128)} %reduce-scatter.2.cloned.1.call-done) | copy-start | bytes 1572868
Sparse Core Ops, SparseCore 0:
  14.2 72.1 all-reduce.4
  165.9 43.0 all-reduce.6
  211.9 35.2 reduce-scatter.1
where the time goes:
time: 311 us; the launch traced here: 307 us
  other arithmetic  123 us (40%)
  waiting for transfers between devices  68.8 us (22%)
  matrix products  42 us (14%)
  blocking collectives  39.4 us (13%)
  between operations  19.7 us (6%)
  local copies, waits for them, and re-layouts  13.7 us (4%)
    psum x1, waiting for transfers between devices, on_device(): inner_sum = jnp.stack([lax.psum(local_inner[0], 'row')])  68.7 us
    psum x1, blocking collectives, on_device(): lax.psum((squares, leader * live_count.astype(jnp.float32)), ('expert', '...  39.4 us
    another operation x7, other arithmetic, on_device(): jnp.linalg.cholesky(jnp.where(refresh_cube, gram_again, identity))  39 us
    another operation x6, other arithmetic, on_device(): jnp.linalg.cholesky(jnp.where(refresh_cube, inner_gram, identity))  34.1 us
    another operation x2, other arithmetic, on_device(): lax.linalg.triangular_solve(lower_second, first_rows, left_side=False, lo...  20 us
    another operation x3, other arithmetic, on_device(): lax.linalg.triangular_solve(lower_first, power_rows.astype(jnp.float32),...  19.7 us
    reduce_sum x1, other arithmetic, on_device(): jnp.sum(jnp.where(live_cube, jnp.square(grads.astype(jnp.float32)), 0.0))  7.48 us
    dot_general x1, matrix products, on_device(): jnp.einsum('cds,cdk->csk', grads, basis, preferred_element_type=jnp.float32)  6.82 us
  transfers between devices with their start and end apart: 3, of which 1 were waited for; matrix products, arithmetic and copies ran while one was open for 29% of the time, Pallas kernels for 0%

commit v1 on v0

--- a/solution.py
+++ b/solution.py
@@ -17,7 +17,7 @@
     squares = jnp.sum(jnp.where(live_cube, jnp.square(grads.astype(jnp.float32)), 0.0))
     leader = (lax.axis_index("row") == 0).astype(jnp.float32)
     total_sq, total_live = lax.psum(
-        (squares, leader * live_count.astype(jnp.float32)), ("expert", "row")
+        lax.psum((squares, leader * live_count.astype(jnp.float32)), "row"), "expert"
     )
     norm_scale = lax.rsqrt(total_sq / (total_live * D * S) + 1e-06)
     local_inner = jnp.einsum("cds,cdk->csk", grads, basis, preferred_element_type=jnp.float32)

time: 311 us -> 299 us (0.961)
  blocking collectives: 39.4 us -> 24.1 us
  waiting for transfers between devices: 68.8 us -> 72.4 us
    psum x1 -> x2, blocking collectives: 39.4 us -> 24.1 us  [the longest x1 14.5 us: on_device(): lax.psum(lax.psum((squares, leader * live_count.astype(jnp.float32)), 'ro...]
    psum x1, waiting for transfers between devices: 0.02 us -> 3.21 us  [on_device(): gram_again = lax.psum(local_second, 'row')]
  transfers between devices with their start and end apart: 3 -> 3, of which waited for: 1 -> 2; matrix products, arithmetic and copies ran while one was open for 29% -> 30% of each run, Pallas kernels for 0% -> 0%
where the time goes in v1:
time: 299 us; the launch traced here: 295 us
  other arithmetic  124 us (41%)
  waiting for transfers between devices  72.4 us (24%)
  matrix products  42 us (14%)
  blocking collectives  24.1 us (8%)
  between operations  19.5 us (7%)
  local copies, waits for them, and re-layouts  13.4 us (4%)
    psum x1, waiting for transfers between devices, on_device(): inner_sum = jnp.stack([lax.psum(local_inner[0], 'row')])  69.1 us
    another operation x7, other arithmetic, on_device(): jnp.linalg.cholesky(jnp.where(refresh_cube, gram_again, identity))  39 us
    another operation x6, other arithmetic, on_device(): jnp.linalg.cholesky(jnp.where(refresh_cube, inner_gram, identity))  34.4 us
    another operation x2, other arithmetic, on_device(): lax.linalg.triangular_solve(lower_second, first_rows, left_side=False, lo...  19.9 us
    another operation x3, other arithmetic, on_device(): lax.linalg.triangular_solve(lower_first, power_rows.astype(jnp.float32),...  19.7 us
    psum x1, blocking collectives, on_device(): lax.psum(lax.psum((squares, leader * live_count.astype(jnp.float32)), 'ro...  14.5 us
    psum x1, blocking collectives, on_device(): lax.psum((squares, leader * live_count.astype(jnp.float32)), 'row')  9.6 us
    reduce_sum x1, other arithmetic, on_device(): jnp.sum(jnp.where(live_cube, jnp.square(grads.astype(jnp.float32)), 0.0))  7.49 us
  transfers between devices with their start and end apart: 3, of which 2 were waited for; matrix products, arithmetic and copies ran while one was open for 30% of the time, Pallas kernels for 0%

profile of v1, /device:TPU:0, one launch (start us, length us, event | category | flops | bytes accessed | tf_op | source)
XLA Modules:
  0.0 295.3 jit_solution(6003827231925301648)
XLA Ops:
  7.2 6.8 %fusion.4 = f32[2048,256]{1,0:T(8,128)} fusion(bf16[1,1792,2048]{2,1,0:T(8,128)(2,1)} %param.9, bf16[1,1792,256]{2,1,0:T(8,128)(2,1)} %param.10), kind=kOutput, calls=%fused_computation.9 | convolution fusion | flops 1879048192 | bytes 10354688 | tf_op jit(solution)/shard_map/cds,cdk->csk/dot_general | solution.py:23
  14.1 1.1 copy-done.2
  15.2 0.8 copy.12
  17.3 69.1 %all-reduce.6.cloned.1.call-done = f32[2048,256]{1,0:T(8,128)} async-done(((f32[2048,256]{1,0:T(8,128)}), f32[2048,256]{1,0:T(8,128)}) %all-reduce.6.cloned.1.call-update) | async-done | bytes 2097168 | tf_op jit(solution)/shard_map/psum | solution.py:24
  86.4 5.7 %convolution_select_fusion = f32[256,256]{0,1:T(8,128)S(1)} fusion(f32[2048,256]{1,0:T(8,128)} %all-reduce.6.cloned.1.call-done, pred[]{:T(512)} %bitcast), kind=kOutput, calls=%fused_computation.32 | convolution fusion | flops 1610809344 | bytes 2359297 | tf_op jit(solution)/shard_map/csk,csj->ckj/dot_general | solution.py:25
  92.3 0.7 copy-done.3
  93.0 11.7 %custom-call.21 = f32[1,128,128]{2,1,0:T(8,128)S(1)} custom-call(f32[1,128,128]{2,1,0:T(8,128)S(1)} %cholesky.191), custom_call_target="Cholesky" | custom-call | tf_op jit(solution)/shard_map/jit(cholesky)/cholesky | solution.py:33
  104.8 9.8 %custom-call.22 = f32[1,1,128,128]{2,3,1,0:T(8,128)S(1)} custom-call(f32[1,1,128,128]{3,2,1,0:T(8,128)S(1)} %get-tuple-element.70), custom_call_target="InvertDiagBlocksLowerTriangular" | custom-call | tf_op jit(solution)/shard_map/jit(cholesky)/cholesky | solution.py:33
  114.6 1.0 bitcast_dynamic-update-slice_fusion.3
  115.7 1.1 fusion.27
  116.8 12.1 %custom-call.23 = f32[1,128,128]{2,1,0:T(8,128)S(1)} custom-call(f32[1,128,128]{2,1,0:T(8,128)S(1)} %fusion.27), custom_call_target="Cholesky" | custom-call | tf_op jit(solution)/shard_map/jit(cholesky)/cholesky | solution.py:33
  128.9 0.7 compare_reduce_fusion.2
  130.9 3.9 %while.8 = (s32[]{:T(128)}, f32[1,256,256]{2,1,0:T(8,128)S(1)}, s32[2,2]{1,0:T(2,128)S(1)}, f32[2,1,128,128]{3,2,1,0:T(8,128)S(1)}, s32[]{:T(128)}) while((s32[]{:T(128)}, f32[1,256,256]{2,1,0:T(8,128)S(1)}, s32[2,2]{1,0:T(2,128)S(1)}, f32[2,1,128,128]{3,2,1,0:T(8,128)S(1)}, s32[]{:T(128)}) %tuple.57), condition=%wide.while_cond, body=%wide.while_body.sunk | while | flops 2 | bytes 131181 | solution.py:34
  131.6 1.4 bitcast_dynamic-update-slice_fusion.6
  133.5 1.4 bitcast_dynamic-update-slice_fusion.6
  134.9 19.7 %custom-call.24 = f32[1,2,128,128]{2,3,1,0:T(8,128)S(1)} custom-call(f32[1,2,128,128]{3,2,1,0:T(8,128)S(1)} %bitcast.221), custom_call_target="InvertDiagBlocksLowerTriangular" | custom-call | tf_op jit(solution)/shard_map/triangular_solve/custom-call.0 | solution.py:34
  154.6 6.2 %fusion.53 = (f32[1,1792,256]{1,2,0:T(8,128)S(1)}, bf16[1,1792,256]{1,2,0:T(8,128)(2,1)}) fusion(bf16[1,1792,2048]{2,1,0:T(8,128)(2,1)} %param.9, f32[2048,256]{1,0:T(8,128)S(1)} %copy-done), kind=kOutput, calls=%fused_computation.99 | convolution fusion | flops 1880489984 | bytes 12189696 | tf_op jit(solution)/shard_map/cds,csk->cdk/dot_general | solution.py:27
  160.8 1.0 fusion.30
  161.7 1.0 fusion.16
  162.7 1.0 convolution_bitcast_fusion.2
  163.7 2.4 fusion.22
  166.3 6.8 %fusion.6 = f32[1,256,2048]{2,1,0:T(8,128)} fusion(bf16[1,1792,2048]{2,1,0:T(8,128)(2,1)} %param.9, bf16[1,1792,256]{1,2,0:T(8,128)(2,1)} %get-tuple-element.72, bf16[1,1792,256]{1,2,0:T(8,128)(2,1)S(1)} %copy.12, pred[]{:T(512)} %bitcast), kind=kOutput, calls=%fused_computation.11 | convolution fusion | flops 1879506944 | bytes 11272193 | tf_op jit(solution)/shard_map/cdk,cds->cks/dot_general | solution.py:31
  173.1 7.5 %select_reduce_fusion = f32[]{:T(128)} fusion(bf16[1,1792,2048]{2,1,0:T(8,128)(2,1)} %param.9, pred[]{:T(512)} %bitcast.40), kind=kLoop, calls=%fused_computation.4 | loop fusion | flops 14680063 | bytes 7340037 | tf_op jit(solution)/shard_map/reduce_sum | solution.py:17
  180.6 9.6 %all-reduce.2 = (f32[]{:T(128)}, f32[]{:T(128)}) all-reduce(f32[]{:T(128)} %select_reduce_fusion, f32[]{:T(128)S(6)} %mul.13), channel_id=1, replica_groups=mesh['expert'=8,'row'=4] {'row'}, use_global_device_ids=true, to_apply=%region_8.12 | all-reduce | flops 2 | bytes 16 | tf_op jit(solution)/shard_map/psum | solution.py:20
  190.2 14.5 %all-reduce.1 = (f32[]{:T(128)}, f32[]{:T(128)}) all-reduce(f32[]{:T(128)} %get-tuple-element.57, f32[]{:T(128)} %get-tuple-element.58), channel_id=1, replica_groups=mesh['expert'=8,'row'=4] {'expert'}, use_global_device_ids=true, to_apply=%region_9.13 | all-reduce | flops 2 | bytes 16 | tf_op jit(solution)/shard_map/psum | solution.py:19
  206.1 3.2 %all-reduce.8.cloned.1.call-done = f32[1,256,256]{1,2,0:T(8,128)} async-done(((f32[1,256,256]{1,2,0:T(8,128)}), f32[1,256,256]{1,2,0:T(8,128)}) %all-reduce.8.cloned.1.call-update) | async-done | bytes 262160 | tf_op jit(solution)/shard_map/psum | solution.py:40
  209.3 1.0 convert_select_fusion
  210.4 1.0 fusion.40
  211.4 12.3 %custom-call.25 = f32[1,128,128]{2,1,0:T(8,128)} custom-call(f32[1,128,128]{2,1,0:T(8,128)S(1)} %cholesky.194), custom_call_target="Cholesky" | custom-call | tf_op jit(solution)/shard_map/jit(cholesky)/cholesky | solution.py:42
  223.7 0.9 cholesky.185
  224.6 1.5 select_reduce_fusion.2
  226.1 11.3 %custom-call.26 = f32[1,1,128,128]{2,3,1,0:T(8,128)} custom-call(f32[1,1,128,128]{3,2,1,0:T(8,128)} %get-tuple-element.66), custom_call_target="InvertDiagBlocksLowerTriangular" | custom-call | tf_op jit(solution)/shard_map/jit(cholesky)/cholesky | solution.py:42
  237.4 1.0 bitcast_dynamic-update-slice_fusion.2
  238.4 0.9 fusion.28
  239.3 12.5 %custom-call.27 = f32[1,128,128]{2,1,0:T(8,128)S(1)} custom-call(f32[1,128,128]{2,1,0:T(8,128)} %fusion.28), custom_call_target="Cholesky" | custom-call | tf_op jit(solution)/shard_map/jit(cholesky)/cholesky | solution.py:42
  251.9 0.6 compare_reduce_fusion
  252.6 0.6 compare_reduce_fusion.1
  254.6 4.0 %while.9 = (s32[]{:T(128)}, f32[1,256,256]{2,1,0:T(8,128)S(1)}, s32[2,2]{1,0:T(2,128)S(1)}, f32[2,1,128,128]{3,2,1,0:T(8,128)S(1)}, s32[]{:T(128)}) while((s32[]{:T(128)}, f32[1,256,256]{2,1,0:T(8,128)S(1)}, s32[2,2]{1,0:T(2,128)S(1)}, f32[2,1,128,128]{3,2,1,0:T(8,128)S(1)}, s32[]{:T(128)}) %tuple.69), condition=%wide.while_cond.clone, body=%wide.while_body.clone.sunk | while | flops 2 | bytes 131181 | solution.py:43
  255.2 1.4 bitcast_dynamic-update-slice_fusion.7
  257.2 1.4 bitcast_dynamic-update-slice_fusion.7
  258.6 19.9 %custom-call.28 = f32[1,2,128,128]{2,3,1,0:T(8,128)S(1)} custom-call(f32[1,2,128,128]{3,2,1,0:T(8,128)S(1)} %bitcast.220), custom_call_target="InvertDiagBlocksLowerTriangular" | custom-call | tf_op jit(solution)/shard_map/triangular_solve/custom-call.0 | solution.py:43
  278.5 0.9 fusion.31
  279.4 1.0 fusion.18
  280.4 1.0 convolution_bitcast_fusion
  281.6 1.7 copy.14
  283.2 1.4 fusion.38
  285.5 1.3 fusion.24
  287.7 0.9 fusion.37
  (45 shorter events, 5.1 us)
Async XLA Ops:
  7.2 79.3 %all-reduce.6.cloned.1.call-start = ((), (), s32[]{:S(2)}) async-start(), calls=%async_computation.1 | async-start | bytes 4194304 | tf_op jit(solution)/shard_map/psum | solution.py:24
  14.0 1.2 copy-start.2
  14.1 195.2 %all-reduce.8.cloned.1.call-start = ((), (), s32[]{:S(2)}) async-start(), calls=%async_computation.2 | async-start | bytes 524288 | tf_op jit(solution)/shard_map/psum | solution.py:40
  92.1 62.5 %copy-start = (f32[2048,256]{1,0:T(8,128)S(1)}, f32[2048,256]{1,0:T(8,128)}, u32[]{:S(2)}) copy-start(f32[2048,256]{1,0:T(8,128)} %all-reduce.6.cloned.1.call-done) | copy-start | bytes 6291460
  92.3 0.7 copy-start.3
  154.6 8.1 %copy-start.4 = (f32[1,2,128,128]{2,3,1,0:T(8,128)}, f32[1,2,128,128]{2,3,1,0:T(8,128)S(1)}, u32[]{:S(2)}) copy-start(f32[1,2,128,128]{2,3,1,0:T(8,128)S(1)} %custom-call.24) | copy-start | bytes 393220
  166.1 117.2 %reduce-scatter.2.cloned.1.call-start = ((), (), s32[]{:S(2)}) async-start(), calls=%async_computation.3 | async-start | bytes 2621440 | tf_op jit(solution)/shard_map/reduce_scatter | solution.py:41
  281.5 1.7 copy-start.5
  283.2 4.4 %copy-start.1 = (f32[1,256,512]{2,1,0:T(8,128)S(1)}, f32[1,256,512]{2,1,0:T(8,128)}, u32[]{:S(2)}) copy-start(f32[1,256,512]{2,1,0:T(8,128)} %reduce-scatter.2.cloned.1.call-done) | copy-start | bytes 1572868
Sparse Core Ops, SparseCore 0:
  14.2 72.1 all-reduce.5
  166.2 43.0 all-reduce.7
  212.2 35.3 reduce-scatter.1
